TPU v7x, 32 devices: a whole 2x2x4 slice. The times are simulated.
32 devices in a mesh: rows: 16 (over z, y, x), sub: 2 (over core).
Axes of the slice: x: 2, y: 2, z: 4, core: 2. Of those that a mesh axis runs over, the one named last changes fastest.
Arguments:
- matrix: float32 [4096, 384], P(('rows', 'sub')), as said below
- grad_out: float32 [4096, 384], P(('rows', 'sub')), as said below
- grad_factor: float32 [384, 384], replicated, may hold values from -6 to 6
Outputs:
- grad_matrix: float32 [4096, 384], P(('rows', 'sub'))
Inputs may be any that keep to these rules, and one draw needn't show every extreme that they name: `matrix`: entries at most of order 1 / sqrt(4096), with a scale that varies by row and by column. `grad_out`: entries of order 0.01.
All inputs are finite; a program needn't handle non-finite values.
Results may differ from a plain program's by a relative error of at most 0.0004.
Values sent between devices are 32-bit elements; how exact they have to be, the bound alone decides.
No kernel may reach another device: no remote copies, remote signals or barrier semaphores. Data moves between devices by JAX's collectives and lax.ppermute only.
A program may use at most 64 MiB of HBM per device.

v0:
```python
import jax
import jax.numpy as jnp
from jax import lax
from jax.sharding import PartitionSpec as P

SECTIONS = 2
shift_frac = 0.02


def full_dot(left, right):
    return jnp.dot(left, right, precision=lax.Precision.HIGHEST, preferred_element_type=jnp.float32)


def inner_gram(left, right):
    return lax.dot_general(
        left,
        right,
        (((0,), (0,)), ((), ())),
        precision=lax.Precision.HIGHEST,
        preferred_element_type=jnp.float32,
    )


def cholesky_adjoint(lower_fac, lower_inv, lower_grad):
    product = full_dot(lower_fac.T, lower_grad)
    phi_part = jnp.tril(product) - 0.5 * jnp.diag(jnp.diag(product))
    sandwich = full_dot(full_dot(lower_inv.T, phi_part), lower_inv)
    return 0.5 * (sandwich + sandwich.T)


def factor_grads(uppers, grad_factor):
    count = len(uppers)
    result = []
    for section_index in range(count):
        middle = grad_factor
        for later in range(section_index + 1, count):
            middle = full_dot(uppers[later].T, middle)
        for earlier in range(section_index - 1, -1, -1):
            middle = full_dot(middle, uppers[earlier].T)
        result.append(middle)
    return result


def summed_gram(partial_value):
    half_rows = lax.psum_scatter(partial_value, "sub", scatter_dimension=0, tiled=True)
    half_rows = lax.psum(half_rows, "rows")
    return lax.all_gather(half_rows, "sub", axis=0, tiled=True)


def per_device(matrix, grad_out, grad_factor):
    width = matrix.shape[1]
    rate = shift_frac / width
    identity = jnp.eye(width, dtype=jnp.float32)
    current = matrix
    saved = []
    for section_index in range(SECTIONS):
        summed = summed_gram(inner_gram(current, current))
        shift_val = rate * jnp.trace(summed)
        lower_fac = jnp.linalg.cholesky(summed + shift_val * identity)
        lower_inv = lax.linalg.triangular_solve(lower_fac, identity, left_side=True, lower=True)
        following = full_dot(current, lower_inv.T)
        saved.append((current, following, lower_fac, lower_inv))
        current = following
    uppers = [item[2].T for item in saved]
    fac_grads = factor_grads(uppers, grad_factor)
    q_grad = grad_out
    for section_index in range(SECTIONS - 1, -1, -1):
        before, after, lower_fac, lower_inv = saved[section_index]
        crossed = lax.psum(inner_gram(after, q_grad), ("rows", "sub"))
        total_grad = fac_grads[section_index] - full_dot(crossed, lower_inv)
        gram_grad = cholesky_adjoint(lower_fac, lower_inv, jnp.tril(total_grad.T))
        gram_grad = gram_grad + rate * jnp.trace(gram_grad) * identity
        q_grad = full_dot(q_grad, lower_inv) + 2.0 * full_dot(before, gram_grad)
    return q_grad


def solution(mesh):
    placed = (P(("rows", "sub"), None), P(("rows", "sub"), None), P())
    return jax.shard_map(
        per_device, mesh=mesh, in_specs=placed, out_specs=P(("rows", "sub"), None), check_vma=False
    )
```

profile of v0, /device:TPU:0, one launch (start us, length us, event | category | flops | bytes accessed | tf_op | source)
XLA Modules:
  0.0 777.9 jit_solution(7228258176599560391)
XLA Ops:
  6.5 2.6 fusion.120
  9.2 11.2 %reduce-scatter.7.cloned.1.call-done = f32[192,384]{1,0:T(8,128)} async-done(((f32[384,384]{1,0:T(8,128)}), f32[192,384]{1,0:T(8,128)}) %reduce-scatter.7.cloned.1.call-update) | async-done | bytes 294928
  22.4 113.0 %all-reduce.6.cloned.1.call-done = f32[192,384]{0,1:T(8,128)} async-done(((f32[192,384]{0,1:T(8,128)}), f32[192,384]{0,1:T(8,128)}) %all-reduce.6.cloned.1.call-update) | async-done | bytes 294928 | tf_op jit(solution)/shard_map/psum | solution.py:46
  140.5 11.7 %cholesky.208 = f32[128,128]{1,0:T(8,128)S(1)} custom-call(f32[128,128]{1,0:T(8,128)S(1)} %cholesky.310), custom_call_target="Cholesky" | custom-call | tf_op jit(solution)/shard_map/jit(cholesky)/cholesky | solution.py:59
  152.3 9.8 %custom-call.24 = f32[1,128,128]{1,2,0:T(8,128)S(1)} custom-call(f32[1,128,128]{2,1,0:T(8,128)S(1)} %get-tuple-element.56), custom_call_target="InvertDiagBlocksLowerTriangular" | custom-call | tf_op jit(solution)/shard_map/jit(cholesky)/cholesky | solution.py:59
  162.7 11.7 %cholesky.227 = f32[128,128]{1,0:T(8,128)S(1)} custom-call(f32[128,128]{1,0:T(8,128)S(1)} %cholesky.314), custom_call_target="Cholesky" | custom-call | tf_op jit(solution)/shard_map/jit(cholesky)/cholesky | solution.py:59
  174.5 10.0 %custom-call.25 = f32[1,128,128]{1,2,0:T(8,128)S(1)} custom-call(f32[1,128,128]{2,1,0:T(8,128)S(1)} %get-tuple-element.53), custom_call_target="InvertDiagBlocksLowerTriangular" | custom-call | tf_op jit(solution)/shard_map/jit(cholesky)/cholesky | solution.py:59
  184.9 11.7 %cholesky.246 = f32[128,128]{1,0:T(8,128)S(1)} custom-call(f32[128,128]{1,0:T(8,128)S(1)} %convolution_subtract_fusion.9), custom_call_target="Cholesky" | custom-call | tf_op jit(solution)/shard_map/jit(cholesky)/cholesky | solution.py:59
  200.0 6.0 while.4
  206.0 29.5 %custom-call.26 = f32[3,128,128]{1,2,0:T(8,128)S(1)} custom-call(f32[3,128,128]{2,1,0:T(8,128)S(1)} %get-tuple-element.21), custom_call_target="InvertDiagBlocksLowerTriangular" | custom-call | tf_op jit(solution)/shard_map/triangular_solve/custom-call.2 | solution.py:60
  240.7 7.1 reduce-scatter.9.cloned.1.call-done
  249.8 112.9 %all-reduce.8.cloned.1.call-done = f32[192,384]{0,1:T(8,128)} async-done(((f32[192,384]{0,1:T(8,128)}), f32[192,384]{0,1:T(8,128)}) %all-reduce.8.cloned.1.call-update) | async-done | bytes 294928 | tf_op jit(solution)/shard_map/psum | solution.py:46
  370.0 11.7 %cholesky.261 = f32[128,128]{1,0:T(8,128)S(1)} custom-call(f32[128,128]{1,0:T(8,128)S(1)} %cholesky.318), custom_call_target="Cholesky" | custom-call | tf_op jit(solution)/shard_map/jit(cholesky)/cholesky | solution.py:59
  381.8 9.8 %custom-call.27 = f32[1,128,128]{1,2,0:T(8,128)S(1)} custom-call(f32[1,128,128]{2,1,0:T(8,128)S(1)} %get-tuple-element.49), custom_call_target="InvertDiagBlocksLowerTriangular" | custom-call | tf_op jit(solution)/shard_map/jit(cholesky)/cholesky | solution.py:59
  392.2 11.7 %cholesky.280 = f32[128,128]{1,0:T(8,128)S(1)} custom-call(f32[128,128]{1,0:T(8,128)S(1)} %cholesky.322), custom_call_target="Cholesky" | custom-call | tf_op jit(solution)/shard_map/jit(cholesky)/cholesky | solution.py:59
  405.3 10.2 %custom-call.28 = f32[1,128,128]{1,2,0:T(8,128)S(1)} custom-call(f32[1,128,128]{2,1,0:T(8,128)S(1)} %get-tuple-element.46), custom_call_target="InvertDiagBlocksLowerTriangular" | custom-call | tf_op jit(solution)/shard_map/jit(cholesky)/cholesky | solution.py:59
  416.0 11.7 %cholesky.299 = f32[128,128]{1,0:T(8,128)S(1)} custom-call(f32[128,128]{1,0:T(8,128)S(1)} %convolution_subtract_fusion.8), custom_call_target="Cholesky" | custom-call | tf_op jit(solution)/shard_map/jit(cholesky)/cholesky | solution.py:59
  431.3 8.7 %while.5 = (s32[]{:T(128)}, f32[384,384]{1,0:T(8,128)}, s32[3,2]{0,1:T(2,128)S(1)}, f32[3,128,128]{2,1,0:T(8,128)S(1)}, s32[]{:T(128)}) while((s32[]{:T(128)}, f32[384,384]{1,0:T(8,128)}, s32[3,2]{0,1:T(2,128)S(1)}, f32[3,128,128]{2,1,0:T(8,128)S(1)}, s32[]{:T(128)}) %tuple.65), condition=%wide.while_cond.clone, body=%wide.while_body.clone.sunk | while | flops 2 | bytes 131181 | solution.py:60
  439.9 29.5 %custom-call.29 = f32[3,128,128]{1,2,0:T(8,128)S(1)} custom-call(f32[3,128,128]{2,1,0:T(8,128)S(1)} %get-tuple-element.22), custom_call_target="InvertDiagBlocksLowerTriangular" | custom-call | tf_op jit(solution)/shard_map/triangular_solve/custom-call.2 | solution.py:60
  480.6 125.3 %all-reduce.10.cloned.1.call-done = f32[384,384]{1,0:T(8,128)} async-done(((f32[384,384]{1,0:T(8,128)}), f32[384,384]{1,0:T(8,128)}) %all-reduce.10.cloned.1.call-update) | async-done | bytes 589840 | tf_op jit(solution)/shard_map/psum | solution.py:69
  611.0 3.4 gather_fusion
  614.4 3.3 fusion.21
  628.1 127.6 %all-reduce.12.cloned.1.call-done = f32[384,384]{1,0:T(8,128)} async-done(((f32[384,384]{1,0:T(8,128)}), f32[384,384]{1,0:T(8,128)}) %all-reduce.12.cloned.1.call-update) | async-done | bytes 589840 | tf_op jit(solution)/shard_map/psum | solution.py:69
  759.8 3.7 gather_fusion.1
  (143 shorter events, 78.1 us)
Async XLA Ops:
  6.5 471.9 %copy-start = (f32[384,384]{1,0:T(8,128)S(1)}, f32[384,384]{1,0:T(8,128)}, u32[]{:S(2)}) copy-start(f32[384,384]{1,0:T(8,128)} %param.8) | copy-start | bytes 1769476
  6.5 13.8 %reduce-scatter.7.cloned.1.call-start = ((), (), s32[]{:S(2)}) async-start(), calls=%async_computation.6 | async-start | bytes 884736
  9.1 126.2 %all-reduce.6.cloned.1.call-start = ((), (), s32[]{:S(2)}) async-start(), calls=%async_computation.2 | async-start | bytes 786432 | tf_op jit(solution)/shard_map/psum | solution.py:46
  22.2 225.6 %reduce-scatter.9.cloned.1.call-start = ((), (), s32[]{:S(2)}) async-start(), calls=%async_computation.7 | async-start | bytes 884736
  22.3 214.5 %copy-start.1 = (f32[384,384]{0,1:T(8,128)}, f32[384,384]{0,1:T(8,128)S(1)}, u32[]{:S(2)}) copy-start(f32[384,384]{0,1:T(8,128)S(1)} %fusion.26) | copy-start | bytes 1769476
  237.6 0.9 copy-start.6
  240.7 122.0 %all-reduce.8.cloned.1.call-start = ((), (), s32[]{:S(2)}) async-start(), calls=%async_computation.3 | async-start | bytes 786432 | tf_op jit(solution)/shard_map/psum | solution.py:46
  249.7 356.1 %all-reduce.10.cloned.1.call-start = ((), (), s32[]{:S(2)}) async-start(), calls=%async_computation.4 | async-start | bytes 1179648 | tf_op jit(solution)/shard_map/psum | solution.py:69
  370.0 11.7 %copy-start.10 = (f32[384,384]{1,0:T(8,128)}, f32[384,384]{1,0:T(8,128)S(1)}, u32[]{:S(2)}) copy-start(f32[384,384]{1,0:T(8,128)S(1)} %fusion.6) | copy-start | bytes 1769476
  381.7 9.9 %copy-start.11 = (f32[384,384]{1,0:T(8,128)S(1)}, f32[384,384]{1,0:T(8,128)}, u32[]{:S(2)}) copy-start(f32[384,384]{1,0:T(8,128)} %copy-done.10) | copy-start | bytes 1769476
  430.4 39.1 %copy-start.2 = (f32[384,384]{0,1:T(8,128)S(1)}, f32[384,384]{0,1:T(8,128)}, u32[]{:S(2)}) copy-start(f32[384,384]{0,1:T(8,128)} %copy-done.1) | copy-start | bytes 1769476
  469.5 0.7 copy-start.14
  475.7 130.2 %copy-start.3 = (f32[128,384]{1,0:T(8,128)}, f32[128,384]{1,0:T(8,128)S(1)}, u32[]{:S(2)}) copy-start(f32[128,384]{1,0:T(8,128)S(1)} %fusion.76) | copy-start | bytes 589828
  475.7 1.0 copy-start.12
  478.2 277.5 %all-reduce.12.cloned.1.call-start = ((), (), s32[]{:S(2)}) async-start(), calls=%async_computation.5 | async-start | bytes 1179648 | tf_op jit(solution)/shard_map/psum | solution.py:69
  614.4 3.3 copy-start.4
  622.3 1.8 copy-start.5
  622.3 1.8 copy-start.13
  625.3 1.5 copy-start.8
  767.1 1.4 copy-start.7
  768.5 0.9 copy-start.9
Sparse Core Ops, SparseCore 0:
  9.6 10.6 reduce-scatter.6
  25.5 109.7 all-reduce.5
  240.8 6.9 reduce-scatter.8
  252.9 109.7 all-reduce.7
  478.4 127.4 all-reduce.9
  626.9 128.7 all-reduce.11
where the time goes:
time: 788 us; the launch traced here: 778 us
  waiting for transfers between devices  497 us (63%)
  other arithmetic  179 us (23%)
  matrix products  43.1 us (5%)
  local copies, waits for them, and re-layouts  33.2 us (4%)
  between operations  20.5 us (3%)
    psum x2, waiting for transfers between devices, per_device(): crossed = lax.psum(inner_gram(after, q_grad), ('rows', 'sub'))  253 us
    psum x2, waiting for transfers between devices, summed_gram(): half_rows = lax.psum(half_rows, 'rows')  226 us
    another operation x21, other arithmetic, per_device(): lower_fac = jnp.linalg.cholesky(summed + shift_val * identity)  114 us
    another operation x5, other arithmetic, per_device(): lax.linalg.triangular_solve(lower_fac, identity, left_side=True, lower=True)  59.9 us
    dot_general x16, matrix products, full_dot(): jnp.dot(left, right, precision=lax.Precision.HIGHEST, preferred_element_t...  25.7 us
    unnamed x8, waiting for transfers between devices  18.4 us
  transfers between devices with their start and end apart: 6, of which 6 were waited for; matrix products, arithmetic and copies ran while one was open for 0% of the time, Pallas kernels for 0%

commit v1 on v0

--- a/solution.py
+++ b/solution.py
@@ -5,6 +5,10 @@
 
 SECTIONS = 2
 shift_frac = 0.02
+
+
+def carry_group_by_axis(a0):
+    return jax.lax.psum(jax.lax.psum(a0, axis_name="sub"), axis_name="rows")
 
 
 def full_dot(left, right):
@@ -66,7 +70,7 @@
     q_grad = grad_out
     for section_index in range(SECTIONS - 1, -1, -1):
         before, after, lower_fac, lower_inv = saved[section_index]
-        crossed = lax.psum(inner_gram(after, q_grad), ("rows", "sub"))
+        crossed = carry_group_by_axis(inner_gram(after, q_grad))
         total_grad = fac_grads[section_index] - full_dot(crossed, lower_inv)
         gram_grad = cholesky_adjoint(lower_fac, lower_inv, jnp.tril(total_grad.T))
         gram_grad = gram_grad + rate * jnp.trace(gram_grad) * identity

time: 788 us -> 800 us (1.015)
  waiting for transfers between devices: 497 us -> 509 us
    psum x2 -> x4, waiting for transfers between devices: 253 us -> 265 us  [carry_group_by_axis(): return jax.lax.psum(jax.lax.psum(a0, axis_name='sub'), axis_name='rows')]
    unnamed x8 -> x10, waiting for transfers between devices: 18.4 us -> 18.4 us
  transfers between devices with their start and end apart: 6 -> 8, of which waited for: 6 -> 8; matrix products, arithmetic and copies ran while one was open for 0% -> 0% of each run, Pallas kernels for 0% -> 0%
where the time goes in v1:
time: 800 us; the launch traced here: 789 us
  waiting for transfers between devices  509 us (64%)
  other arithmetic  179 us (22%)
  matrix products  43 us (5%)
  local copies, waits for them, and re-layouts  32.9 us (4%)
  between operations  20.4 us (3%)
    psum x4, waiting for transfers between devices, carry_group_by_axis(): return jax.lax.psum(jax.lax.psum(a0, axis_name='sub'), axis_name='rows')  265 us
    psum x2, waiting for transfers between devices, summed_gram(): half_rows = lax.psum(half_rows, 'rows')  226 us
    another operation x21, other arithmetic, per_device(): lower_fac = jnp.linalg.cholesky(summed + shift_val * identity)  114 us
    another operation x5, other arithmetic, per_device(): lax.linalg.triangular_solve(lower_fac, identity, left_side=True, lower=True)  59.9 us
    dot_general x16, matrix products, full_dot(): jnp.dot(left, right, precision=lax.Precision.HIGHEST, preferred_element_t...  25.6 us
    unnamed x10, waiting for transfers between devices  18.4 us
  transfers between devices with their start and end apart: 8, of which 8 were waited for; matrix products, arithmetic and copies ran while one was open for 0% of the time, Pallas kernels for 0%

profile of v1, /device:TPU:0, one launch (start us, length us, event | category | flops | bytes accessed | tf_op | source)
XLA Modules:
  0.0 789.3 jit_solution(16242251197540875857)
XLA Ops:
  9.2 11.2 %reduce-scatter.7.cloned.1.call-done = f32[192,384]{1,0:T(8,128)} async-done(((f32[384,384]{1,0:T(8,128)}), f32[192,384]{1,0:T(8,128)}) %reduce-scatter.7.cloned.1.call-update) | async-done | bytes 294928
  22.4 113.0 %all-reduce.8.cloned.1.call-done = f32[192,384]{0,1:T(8,128)} async-done(((f32[192,384]{0,1:T(8,128)}), f32[192,384]{0,1:T(8,128)}) %all-reduce.8.cloned.1.call-update) | async-done | bytes 294928 | tf_op jit(solution)/shard_map/psum | solution.py:50
  140.5 11.7 %cholesky.208 = f32[128,128]{1,0:T(8,128)S(1)} custom-call(f32[128,128]{1,0:T(8,128)S(1)} %cholesky.310), custom_call_target="Cholesky" | custom-call | tf_op jit(solution)/shard_map/jit(cholesky)/cholesky | solution.py:63
  152.3 9.8 %custom-call.24 = f32[1,128,128]{1,2,0:T(8,128)S(1)} custom-call(f32[1,128,128]{2,1,0:T(8,128)S(1)} %get-tuple-element.56), custom_call_target="InvertDiagBlocksLowerTriangular" | custom-call | tf_op jit(solution)/shard_map/jit(cholesky)/cholesky | solution.py:63
  162.7 11.7 %cholesky.227 = f32[128,128]{1,0:T(8,128)S(1)} custom-call(f32[128,128]{1,0:T(8,128)S(1)} %cholesky.314), custom_call_target="Cholesky" | custom-call | tf_op jit(solution)/shard_map/jit(cholesky)/cholesky | solution.py:63
  174.5 10.2 %custom-call.25 = f32[1,128,128]{1,2,0:T(8,128)S(1)} custom-call(f32[1,128,128]{2,1,0:T(8,128)S(1)} %get-tuple-element.53), custom_call_target="InvertDiagBlocksLowerTriangular" | custom-call | tf_op jit(solution)/shard_map/jit(cholesky)/cholesky | solution.py:63
  185.2 11.7 %cholesky.246 = f32[128,128]{1,0:T(8,128)S(1)} custom-call(f32[128,128]{1,0:T(8,128)S(1)} %convolution_subtract_fusion.9), custom_call_target="Cholesky" | custom-call | tf_op jit(solution)/shard_map/jit(cholesky)/cholesky | solution.py:63
  200.3 6.0 while.4
  206.3 29.5 %custom-call.26 = f32[3,128,128]{1,2,0:T(8,128)S(1)} custom-call(f32[3,128,128]{2,1,0:T(8,128)S(1)} %get-tuple-element.21), custom_call_target="InvertDiagBlocksLowerTriangular" | custom-call | tf_op jit(solution)/shard_map/triangular_solve/custom-call.2 | solution.py:64
  241.0 7.1 reduce-scatter.9.cloned.1.call-done
  250.1 112.9 %all-reduce.10.cloned.1.call-done = f32[192,384]{0,1:T(8,128)} async-done(((f32[192,384]{0,1:T(8,128)}), f32[192,384]{0,1:T(8,128)}) %all-reduce.10.cloned.1.call-update) | async-done | bytes 294928 | tf_op jit(solution)/shard_map/psum | solution.py:50
  370.2 11.7 %cholesky.261 = f32[128,128]{1,0:T(8,128)S(1)} custom-call(f32[128,128]{1,0:T(8,128)S(1)} %cholesky.318), custom_call_target="Cholesky" | custom-call | tf_op jit(solution)/shard_map/jit(cholesky)/cholesky | solution.py:63
  382.0 9.8 %custom-call.27 = f32[1,128,128]{1,2,0:T(8,128)S(1)} custom-call(f32[1,128,128]{2,1,0:T(8,128)S(1)} %get-tuple-element.49), custom_call_target="InvertDiagBlocksLowerTriangular" | custom-call | tf_op jit(solution)/shard_map/jit(cholesky)/cholesky | solution.py:63
  392.4 11.7 %cholesky.280 = f32[128,128]{1,0:T(8,128)S(1)} custom-call(f32[128,128]{1,0:T(8,128)S(1)} %cholesky.322), custom_call_target="Cholesky" | custom-call | tf_op jit(solution)/shard_map/jit(cholesky)/cholesky | solution.py:63
  405.4 10.0 %custom-call.28 = f32[1,128,128]{1,2,0:T(8,128)S(1)} custom-call(f32[1,128,128]{2,1,0:T(8,128)S(1)} %get-tuple-element.46), custom_call_target="InvertDiagBlocksLowerTriangular" | custom-call | tf_op jit(solution)/shard_map/jit(cholesky)/cholesky | solution.py:63
  415.9 11.7 %cholesky.299 = f32[128,128]{1,0:T(8,128)S(1)} custom-call(f32[128,128]{1,0:T(8,128)S(1)} %convolution_subtract_fusion.8), custom_call_target="Cholesky" | custom-call | tf_op jit(solution)/shard_map/jit(cholesky)/cholesky | solution.py:63
  431.2 8.7 %while.5 = (s32[]{:T(128)}, f32[384,384]{1,0:T(8,128)}, s32[3,2]{0,1:T(2,128)S(1)}, f32[3,128,128]{2,1,0:T(8,128)S(1)}, s32[]{:T(128)}) while((s32[]{:T(128)}, f32[384,384]{1,0:T(8,128)}, s32[3,2]{0,1:T(2,128)S(1)}, f32[3,128,128]{2,1,0:T(8,128)S(1)}, s32[]{:T(128)}) %tuple.69), condition=%wide.while_cond.clone, body=%wide.while_body.clone.sunk | while | flops 2 | bytes 131181 | solution.py:64
  439.9 29.5 %custom-call.29 = f32[3,128,128]{1,2,0:T(8,128)S(1)} custom-call(f32[3,128,128]{2,1,0:T(8,128)S(1)} %get-tuple-element.22), custom_call_target="InvertDiagBlocksLowerTriangular" | custom-call | tf_op jit(solution)/shard_map/triangular_solve/custom-call.2 | solution.py:64
  478.2 17.8 %all-reduce.12.cloned.1.call-done = f32[384,384]{1,0:T(8,128)} async-done(((f32[384,384]{1,0:T(8,128)}), f32[384,384]{1,0:T(8,128)}) %all-reduce.12.cloned.1.call-update) | async-done | bytes 589840 | tf_op jit(solution)/shard_map/psum | solution.py:11
  498.6 113.8 %all-reduce.14.cloned.1.call-done = f32[384,384]{1,0:T(8,128)} async-done(((f32[384,384]{1,0:T(8,128)}), f32[384,384]{1,0:T(8,128)}) %all-reduce.14.cloned.1.call-update) | async-done | bytes 589840 | tf_op jit(solution)/shard_map/psum | solution.py:11
  617.5 3.4 gather_fusion
  633.6 17.6 %all-reduce.16.cloned.1.call-done = f32[384,384]{1,0:T(8,128)} async-done(((f32[384,384]{1,0:T(8,128)}), f32[384,384]{1,0:T(8,128)}) %all-reduce.16.cloned.1.call-update) | async-done | bytes 589840 | tf_op jit(solution)/shard_map/psum | solution.py:11
  652.5 115.3 %all-reduce.18.cloned.1.call-done = f32[384,384]{1,0:T(8,128)} async-done(((f32[384,384]{1,0:T(8,128)}), f32[384,384]{1,0:T(8,128)}) %all-reduce.18.cloned.1.call-update) | async-done | bytes 589840 | tf_op jit(solution)/shard_map/psum | solution.py:11
  771.9 3.4 gather_fusion.1
  (141 shorter events, 84.1 us)
Async XLA Ops:
  6.5 490.0 %copy-start = (f32[384,384]{1,0:T(8,128)S(1)}, f32[384,384]{1,0:T(8,128)}, u32[]{:S(2)}) copy-start(f32[384,384]{1,0:T(8,128)} %param.8) | copy-start | bytes 1769476
  6.5 13.8 %reduce-scatter.7.cloned.1.call-start = ((), (), s32[]{:S(2)}) async-start(), calls=%async_computation.8 | async-start | bytes 884736
  9.1 126.2 %all-reduce.8.cloned.1.call-start = ((), (), s32[]{:S(2)}) async-start(), calls=%async_computation.2 | async-start | bytes 786432 | tf_op jit(solution)/shard_map/psum | solution.py:50
  22.2 225.9 %reduce-scatter.9.cloned.1.call-start = ((), (), s32[]{:S(2)}) async-start(), calls=%async_computation.9 | async-start | bytes 884736
  22.3 214.8 %copy-start.1 = (f32[384,384]{0,1:T(8,128)}, f32[384,384]{0,1:T(8,128)S(1)}, u32[]{:S(2)}) copy-start(f32[384,384]{0,1:T(8,128)S(1)} %fusion.26) | copy-start | bytes 1769476
  237.9 0.9 copy-start.6
  241.0 122.0 %all-reduce.10.cloned.1.call-start = ((), (), s32[]{:S(2)}) async-start(), calls=%async_computation.3 | async-start | bytes 786432 | tf_op jit(solution)/shard_map/psum | solution.py:50
  250.0 246.0 %all-reduce.12.cloned.1.call-start = ((), (), s32[]{:S(2)}) async-start(), calls=%async_computation.4 | async-start | bytes 1179648 | tf_op jit(solution)/shard_map/psum | solution.py:11
  430.3 39.1 %copy-start.2 = (f32[384,384]{0,1:T(8,128)S(1)}, f32[384,384]{0,1:T(8,128)}, u32[]{:S(2)}) copy-start(f32[384,384]{0,1:T(8,128)} %copy-done.1) | copy-start | bytes 1769476
  469.4 0.7 copy-start.10
  475.6 136.8 %copy-start.3 = (f32[128,384]{1,0:T(8,128)}, f32[128,384]{1,0:T(8,128)S(1)}, u32[]{:S(2)}) copy-start(f32[128,384]{1,0:T(8,128)S(1)} %fusion.76) | copy-start | bytes 589828
  475.6 1.0 copy-start.8
  478.1 134.3 %all-reduce.14.cloned.1.call-start = ((), (), s32[]{:S(2)}) async-start(), calls=%async_computation.5 | async-start | bytes 1179648 | tf_op jit(solution)/shard_map/psum | solution.py:11
  496.0 155.2 %all-reduce.16.cloned.1.call-start = ((), (), s32[]{:S(2)}) async-start(), calls=%async_computation.6 | async-start | bytes 1179648 | tf_op jit(solution)/shard_map/psum | solution.py:11
  620.9 3.3 copy-start.4
  628.9 1.8 copy-start.5
  628.9 1.8 copy-start.9
  633.3 134.4 %all-reduce.18.cloned.1.call-start = ((), (), s32[]{:S(2)}) async-start(), calls=%async_computation.7 | async-start | bytes 1179648 | tf_op jit(solution)/shard_map/psum | solution.py:11
  778.9 1.3 copy-start.7
Sparse Core Ops, SparseCore 0:
  9.6 10.6 reduce-scatter.6
  25.5 109.7 all-reduce.7
  241.1 6.9 reduce-scatter.8
  253.1 109.7 all-reduce.9
  478.2 17.7 all-reduce.11
  501.2 111.1 all-reduce.13
  633.5 17.6 all-reduce.15
  656.5 111.2 all-reduce.17
